TPU v7x, 256 devices: a whole 4x4x8 slice. The times are simulated.
256 devices in a mesh: dp: 256 (over y, z, x, core).
Axes of the slice: x: 4, y: 4, z: 8, core: 2. Of those that a mesh axis runs over, the one named last changes fastest.
Arguments:
- master: float32 [524288], P('dp'), may hold values from -6 to 6
- gradients: float32 [524288], P('dp'), may hold values from -6 to 6
- first_moment: float32 [524288], P('dp'), may hold values from -4 to 4
- second_moment: float32 [524288], P('dp'), may hold values from 0.01 to 1
- segment_ids: int32 [524288], P('dp'), may hold values from 0 to 511, as said below
- decay_mask: int32 [512], replicated, may hold values 0 or 1
Outputs:
- new_master: float32 [524288], P('dp')
- new_first: float32 [524288], P('dp')
- new_second: float32 [524288], P('dp')
- scaled_step: float32 [524288], P('dp')
- model_weights: bfloat16 [524288], replicated
Inputs may be any that keep to these rules, and one draw needn't show every extreme that they name: segment_ids never falls along the flat vector; each tensor 0 to 511 owns one contiguous run of 256 to 16384 elements, and one tensor has exactly 16384. `decay_mask`: each entry is 0 or 1.
All inputs are finite; a program needn't handle non-finite values.
Results may differ from a plain program's by a relative error of at most 0.0004.
Values may be sent and summed in bfloat16 or wider, within the bound.
A program may use at most 64 MiB of HBM per device.

v0:
```python
import functools
import math

import jax
import jax.numpy as jnp
from jax import lax
from jax.sharding import Mesh
from jax.sharding import PartitionSpec as P

SEG_DEV = 2
STEP = 20
DP = ("dp_0", "dp_1", "dp_2", "dp_3")


first_decay = 0.9
second_decay = 0.999
epsilon = 1e-06
weight_decay = 0.01
learn_rate = 0.006


def one_axis_at_a_time(value, axes):
    return functools.reduce(lax.psum, axes, value)


def adam_direction(master, gradients, first_moment, second_moment, decay):
    new_first = first_decay * first_moment + (1.0 - first_decay) * gradients
    new_second = second_decay * second_moment + (1.0 - second_decay) * gradients * gradients
    hat_first = new_first / (1.0 - first_decay**STEP)
    hat_second = new_second / (1.0 - second_decay**STEP)
    direction = hat_first / (jnp.sqrt(hat_second) + epsilon) + weight_decay * decay * master
    return (new_first, new_second, direction)


def trust_ratio(weight_sq, step_sq):
    weight_norm = jnp.sqrt(weight_sq)
    step_norm = jnp.sqrt(step_sq)
    usable = (weight_norm > 0.0) & (step_norm > 0.0)
    return jnp.where(usable, weight_norm / jnp.where(usable, step_norm, 1.0), 1.0)


def block_rows(length):
    return math.gcd(length, 1024)


def one_hot_block(ids, width):
    columns = lax.broadcasted_iota(jnp.int32, (ids.shape[0], width), 1)
    return (ids[:, None] == columns).astype(jnp.float32)


def spread(table, ids, width):
    length = ids.shape[0]
    rows = block_rows(length)
    blocks = ids.reshape(length // rows, rows)

    def one_block(block_ids):
        return jnp.dot(one_hot_block(block_ids, width), table, precision=lax.Precision.HIGHEST)

    return lax.map(one_block, blocks).reshape(length, table.shape[1])


def collect(values, ids, width):
    length = ids.shape[0]
    rows = block_rows(length)
    blocks = ids.reshape(length // rows, rows)
    value_blocks = values.reshape(length // rows, rows, values.shape[1])

    def add_block(total, pair):
        block_ids, block_values = pair
        term = lax.dot_general(
            one_hot_block(block_ids, width),
            block_values,
            (((0,), (0,)), ((), ())),
            precision=lax.Precision.HIGHEST,
        )
        return (total + term, None)

    start = jnp.zeros((width, values.shape[1]), jnp.float32)
    total, unused = lax.scan(add_block, start, (blocks, value_blocks))
    return total


def to_global(partial_value, first_id, tensors, width):
    holder = jnp.zeros((tensors + width, partial_value.shape[1]), jnp.float32)
    placed = lax.dynamic_update_slice_in_dim(holder, partial_value, first_id, 0)
    return placed[:tensors]


def to_local(table, first_id, width, filler):
    padded = jnp.concatenate([table, jnp.full((width,), filler, jnp.float32)])
    return lax.dynamic_slice_in_dim(padded, first_id, width)


def shards(master, gradients, first_moment, second_moment, segment_ids, decay_mask):
    tensors = decay_mask.shape[0]
    width = 4 * SEG_DEV + 2
    first_id = segment_ids[0].astype(jnp.int32)
    local_ids = (segment_ids - first_id).astype(jnp.int32)
    local_mask = to_local(decay_mask.astype(jnp.float32), first_id, width, 0.0)
    decay = spread(local_mask[:, None], local_ids, width)[:, 0]
    weight_square = master * master
    new_first, new_second, direction = adam_direction(
        master, gradients, first_moment, second_moment, decay
    )
    stacked = jnp.stack([weight_square, direction * direction], axis=1)
    packed_partial = to_global(collect(stacked, local_ids, width), first_id, tensors, width)
    totals = one_axis_at_a_time(packed_partial, DP)
    ratios = to_local(trust_ratio(totals[:, 0], totals[:, 1]), first_id, width, 1.0)
    per_element = spread(ratios[:, None], local_ids, width)[:, 0]
    scaled_step = per_element * direction
    new_master = master - learn_rate * scaled_step
    model_weights = lax.all_gather(new_master.astype(jnp.bfloat16), DP, axis=0, tiled=True)
    return (new_master, new_first, new_second, scaled_step, model_weights)


def solution(mesh):
    torus = Mesh(mesh.devices.reshape(4, 8, 4, 2), ("dp_0", "dp_1", "dp_2", "dp_3"))
    return jax.shard_map(
        shards,
        mesh=torus,
        in_specs=(P(DP), P(DP), P(DP), P(DP), P(DP), P()),
        out_specs=(P(DP), P(DP), P(DP), P(DP), P()),
        check_vma=False,
    )
```

profile of v0, /device:TPU:1, one launch (start us, length us, event | category | flops | bytes accessed | tf_op | source)
XLA Modules:
  0.0 167.0 jit_solution(12047578045685534841)
XLA Ops:
  7.2 0.0 all-gather.2.cloned.1.call-start
  7.2 1.2 slice.12
  9.1 0.7 broadcast_subtract_fusion
  11.1 0.1 fusion.10
  11.2 1.0 while.31
  11.2 0.5 fusion.23
  11.7 0.5 fusion.23
  12.2 0.7 copy-done
  12.9 0.6 fusion.13
  13.5 0.8 while.33
  13.6 0.4 convolution_add_fusion.2
  14.0 0.4 convolution_add_fusion.2
  14.4 0.3 dynamic_update_slice.10
  14.7 9.6 %psum.28 = f32[512,2]{0,1:T(2,128)S(1)} all-reduce(f32[512,2]{0,1:T(2,128)S(1)} %slice.16), channel_id=1, replica_groups=mesh['dp_0'=4,'dp_1'=8,'dp_2'=4,'dp_3'=2] {'dp_0'}, use_global_device_ids=true, to_apply=%region_4.5 | all-reduce | flops 1024 | bytes 8192 | tf_op jit(solution)/shard_map/psum | solution.py:23
  24.2 16.2 %psum.29 = f32[512,2]{0,1:T(2,128)S(1)} all-reduce(f32[512,2]{0,1:T(2,128)S(1)} %psum.28), channel_id=1, replica_groups=mesh['dp_0'=4,'dp_1'=8,'dp_2'=4,'dp_3'=2] {'dp_1'}, use_global_device_ids=true, to_apply=%region_5.6 | all-reduce | flops 1024 | bytes 8192 | tf_op jit(solution)/shard_map/psum | solution.py:23
  40.5 8.5 %psum.30 = f32[512,2]{0,1:T(2,128)S(1)} all-reduce(f32[512,2]{0,1:T(2,128)S(1)} %psum.29), channel_id=1, replica_groups=mesh['dp_0'=4,'dp_1'=8,'dp_2'=4,'dp_3'=2] {'dp_2'}, use_global_device_ids=true, to_apply=%region_6.7 | all-reduce | flops 1024 | bytes 8192 | tf_op jit(solution)/shard_map/psum | solution.py:23
  48.9 10.6 %psum.31 = f32[512,2]{0,1:T(2,128)S(1)} all-reduce(f32[512,2]{0,1:T(2,128)S(1)} %psum.30), channel_id=1, replica_groups=mesh['dp_0'=4,'dp_1'=8,'dp_2'=4,'dp_3'=2] {'dp_3'}, use_global_device_ids=true, to_apply=%region_7.8 | all-reduce | flops 1024 | bytes 8192 | tf_op jit(solution)/shard_map/psum | solution.py:23
  59.5 0.1 fusion.11
  59.6 0.9 while.32
  59.6 0.5 fusion.25
  60.1 0.5 fusion.25
  60.6 0.6 fusion.12
  61.2 96.7 %all-gather.2.cloned.1.call-done = bf16[524288]{0:T(1024)(128)(2,1)} async-done(((bf16[2048]{0:T(1024)(128)(2,1)}), bf16[524288]{0:T(1024)(128)(2,1)}) %all-gather.2.cloned.1.call-update) | async-done | bytes 1048592 | tf_op jit(solution)/shard_map/all_gather | solution.py:112
  157.9 2.3 %copy.35 = bf16[524288]{0:T(1024)(128)(2,1)} copy(bf16[524288]{0:T(1024)(128)(2,1)} %all-gather.2.cloned.1.call-done) | data formatting | bytes 2097152
  (29 shorter events, 0.2 us)
Async XLA Ops:
  7.2 1.9 %copy-start.4 = (s32[2048]{0:T(1024)S(1)}, s32[2048]{0:T(1024)}, u32[]{:S(2)}) copy-start(s32[2048]{0:T(1024)} %param.16) | copy-start | bytes 24580
  7.2 150.7 %all-gather.2.cloned.1.call-start = ((), (), s32[]{:S(2)}) async-start(), calls=%async_computation | async-start | bytes 1052672 | tf_op jit(solution)/shard_map/all_gather | solution.py:112
  9.1 1.3 copy-start.5
  11.2 1.0 copy-start.2
  11.2 1.0 copy-start.3
  12.2 0.7 copy-start
  12.2 0.7 copy-start.1
Sparse Core Ops, SparseCore 0:
  61.4 96.5 all-gather.1
where the time goes:
time: 167 us
  waiting for transfers between devices  96.7 us (58%)
  blocking collectives  44.9 us (27%)
  between operations  16.1 us (10%)
  local copies, waits for them, and re-layouts  4.7 us (3%)
  matrix products  2.58 us (2%)
  other arithmetic  1.93 us (1%)
    all_gather x1, waiting for transfers between devices, shards(): lax.all_gather(new_master.astype(jnp.bfloat16), DP, axis=0, tiled=True)  96.7 us
    psum x4, blocking collectives, one_axis_at_a_time(): return functools.reduce(lax.psum, axes, value)  44.9 us
  transfers between devices with their start and end apart: 1, of which 1 were waited for; matrix products, arithmetic and copies ran while one was open for 0% of the time, Pallas kernels for 0%

commit v1 on v0

v1 whole, which is shorter than its diff:
```python
import functools

import jax
import jax.numpy as jnp
from jax import lax
from jax.experimental import pallas as pl
from jax.experimental.pallas import tpu as pltpu
from jax.sharding import PartitionSpec as P

STEP = 20
first_decay = 0.9
second_decay = 0.999
epsilon = 1e-06
weight_decay = 0.01
learn_rate = 0.006

NY, NZ, NX, NC = 4, 8, 4, 2
DEVICES = NY * NZ * NX * NC
ROWS, LANES = 16, 128
REACH = 8
SEGMENTS = 9
MESH = pl.DeviceIdType.MESH


def adam_direction(master, gradients, first_moment, second_moment, decay):
    new_first = first_decay * first_moment + (1.0 - first_decay) * gradients
    new_second = second_decay * second_moment + (1.0 - second_decay) * gradients * gradients
    hat_first = new_first / (1.0 - first_decay**STEP)
    hat_second = new_second / (1.0 - second_decay**STEP)
    direction = hat_first / (jnp.sqrt(hat_second) + epsilon) + weight_decay * decay * master
    return (new_first, new_second, direction)


def trust_ratio(weight_sq, step_sq):
    weight_norm = jnp.sqrt(weight_sq)
    step_norm = jnp.sqrt(step_sq)
    usable = (weight_norm > 0.0) & (step_norm > 0.0)
    return jnp.where(usable, weight_norm / jnp.where(usable, step_norm, 1.0), 1.0)


def total_of(values):
    return jnp.sum(jnp.sum(values, axis=0, keepdims=True), axis=1, keepdims=True)


def kernel(
    master_hbm, grad_hbm, first_hbm, second_hbm, ids_hbm, mask_hbm,
    new_master_ref, new_first_ref, new_second_ref, scaled_ref, gathered,
    master_ref, grad_ref, first_ref, second_ref, ids_ref, ids_smem, mask_smem,
    outgoing, incoming,
    in_sems, stat_send, stat_recv, z_send, z_recv, p_send, p_recv, q_send, q_recv, d_send, d_recv,
):
    me = lax.axis_index("dp")
    c = lax.rem(me, 2)
    x = lax.rem(me // 2, NX)
    z = lax.rem(me // 8, NZ)
    y = me // 64

    def device(yy, zz, xx, cc):
        return ((yy * NZ + zz) * NX + xx) * NC + cc

    def shifted(offset):
        return lax.rem(me + offset + DEVICES, DEVICES)

    class_a = 1 - c

    def p_peer(k):
        return device(
            lax.rem(y + class_a * k, NY), z, lax.rem(x + c * k, NX), c
        )

    def q_peer(k):
        return device(
            lax.rem(y + c * k, NY), z, lax.rem(x + class_a * k, NX), c
        )

    def column(core, pj, qk):
        a = 1 - core
        yy = lax.rem(y + a * pj + core * qk, NY)
        xx = lax.rem(x + core * pj + a * qk, NX)
        return gathered.at[yy, :, xx, core]

    z_peers = [device(y, lax.rem(z + k, NZ), x, c) for k in range(1, NZ)]
    p_peers = [p_peer(k) for k in range(1, 4)]
    q_peers = [q_peer(k) for k in range(1, 4)]
    sibling = device(y, z, x, 1 - c)
    up = [shifted(k) for k in range(1, REACH + 1)]
    down = [shifted(-k) for k in range(1, REACH + 1)]

    barrier = pltpu.get_barrier_semaphore()
    partners = up + down + z_peers + p_peers + q_peers + [sibling]
    for partner in partners:
        pl.semaphore_signal(barrier, inc=1, device_id=(partner,), device_id_type=MESH)

    loads = [
        pltpu.make_async_copy(src, dst, in_sems.at[i])
        for i, (src, dst) in enumerate(
            [
                (ids_hbm, ids_smem),
                (mask_hbm, mask_smem),
                (ids_hbm, ids_ref),
                (master_hbm, master_ref),
                (grad_hbm, grad_ref),
                (first_hbm, first_ref),
                (second_hbm, second_ref),
            ]
        )
    ]
    for load in loads:
        load.start()
    for load in loads:
        load.wait()

    first_id = ids_smem[0, 0]
    last_id = ids_smem[ROWS - 1, LANES - 1]
    last_local = last_id - first_id
    local = ids_ref[...] - first_id
    decay = jnp.zeros((ROWS, LANES), jnp.float32)
    for k in range(SEGMENTS):
        value = mask_smem[jnp.minimum(first_id + k, mask_smem.shape[0] - 1)]
        decay = jnp.where(local == k, value.astype(jnp.float32), decay)

    master = master_ref[...]
    new_first, new_second, direction = adam_direction(
        master, grad_ref[...], first_ref[...], second_ref[...], decay
    )
    new_first_ref[...] = new_first
    new_second_ref[...] = new_second
    weight_square = master * master
    step_square = direction * direction

    def masked(index):
        hit = local == index
        return (
            total_of(jnp.where(hit, weight_square, 0.0)),
            total_of(jnp.where(hit, step_square, 0.0)),
        )

    head_w, head_s = masked(0)
    tail_w, tail_s = masked(last_local)
    shape = (1, LANES)
    for slot, (key, w, s) in enumerate(
        [(last_id, tail_w, tail_s), (first_id, head_w, head_s)]
    ):
        outgoing[slot, 0:1, :] = jnp.full(shape, key.astype(jnp.float32))
        outgoing[slot, 1:2, :] = jnp.broadcast_to(w, shape)
        outgoing[slot, 2:3, :] = jnp.broadcast_to(s, shape)

    pl.semaphore_wait(barrier, len(partners))

    stats = []
    for k in range(REACH):
        for way, peers in ((0, up), (1, down)):
            slot = way * REACH + k
            copy = pltpu.make_async_remote_copy(
                src_ref=outgoing.at[way],
                dst_ref=incoming.at[slot],
                send_sem=stat_send.at[slot],
                recv_sem=stat_recv.at[slot],
                device_id=(peers[k],),
                device_id_type=MESH,
            )
            copy.start()
            stats.append(copy)

    trust = jnp.ones((ROWS, LANES), jnp.float32)
    for k in range(1, SEGMENTS - 1):
        w, s = masked(k)
        trust = jnp.where(local == k, trust_ratio(w, s), trust)

    for copy in stats:
        copy.wait_recv()
    sums = [jnp.broadcast_to(v, shape) for v in (head_w, head_s, tail_w, tail_s)]
    for key, base in ((first_id, 0), (last_id, 2)):
        target = key.astype(jnp.float32)
        for slot in range(2 * REACH):
            hit = incoming[slot, 0:1, :] == target
            sums[base] += jnp.where(hit, incoming[slot, 1:2, :], 0.0)
            sums[base + 1] += jnp.where(hit, incoming[slot, 2:3, :], 0.0)
    trust = jnp.where(local == last_local, trust_ratio(sums[2], sums[3]), trust)
    trust = jnp.where(local == 0, trust_ratio(sums[0], sums[1]), trust)

    scaled = trust * direction
    new_master = master - learn_rate * scaled
    gathered[y, z, x, c] = new_master.astype(jnp.bfloat16)

    def send(block, send_sem, recv_sem, peer):
        copy = pltpu.make_async_remote_copy(
            src_ref=block,
            dst_ref=block,
            send_sem=send_sem,
            recv_sem=recv_sem,
            device_id=(peer,),
            device_id_type=MESH,
        )
        copy.start()
        return copy

    def arrived(block, send_sem, recv_sem):
        pltpu.make_async_remote_copy(
            src_ref=block,
            dst_ref=block,
            send_sem=send_sem,
            recv_sem=recv_sem,
            device_id=(me,),
            device_id_type=MESH,
        ).wait_recv()

    sends = []
    own = gathered.at[y, z, x, c]
    for k in (4, 3, 5, 2, 6, 1, 7):
        sends.append(send(own, z_send.at[k - 1], z_recv.at[k - 1], z_peers[k - 1]))
    new_master_ref[...] = new_master
    scaled_ref[...] = scaled
    for k in (7, 1, 6, 2, 5, 3, 4):
        arrived(
            gathered.at[y, lax.rem(z + NZ - k, NZ), x, c], z_send.at[k - 1], z_recv.at[k - 1]
        )

    mine = column(c, 0, 0)
    for k in (2, 1, 3):
        sends.append(send(mine, p_send.at[k - 1], p_recv.at[k - 1], p_peers[k - 1]))

    def spread_block(j):
        block = column(c, j, 0)
        for k in (2, 1, 3):
            slot = j * 3 + k - 1
            sends.append(send(block, q_send.at[slot], q_recv.at[slot], q_peers[k - 1]))
        sends.append(send(block, d_send.at[j * 4], d_recv.at[j * 4], sibling))

    spread_block(0)
    for k in (1, 3, 2):
        j = 4 - k
        arrived(column(c, j, 0), p_send.at[k - 1], p_recv.at[k - 1])
        spread_block(j)
    for j in (0, 3, 1, 2):
        for k in (1, 3, 2):
            slot = j * 3 + k - 1
            block = column(c, j, 4 - k)
            arrived(block, q_send.at[slot], q_recv.at[slot])
            label = j * 4 + 4 - k
            sends.append(send(block, d_send.at[label], d_recv.at[label], sibling))
    for j in range(4):
        for k in range(4):
            label = j * 4 + k
            arrived(column(1 - c, j, k), d_send.at[label], d_recv.at[label])
    for copy in stats:
        copy.wait_send()
    for copy in sends:
        copy.wait_send()


def shards(master, gradients, first_moment, second_moment, segment_ids, decay_mask):
    tile = (ROWS, LANES)
    f32 = jax.ShapeDtypeStruct(tile, jnp.float32)
    dma = pltpu.SemaphoreType.DMA
    outs = pl.pallas_call(
        kernel,
        out_shape=[f32, f32, f32, f32,
                   jax.ShapeDtypeStruct((NY, NZ, NX, NC, ROWS, LANES), jnp.bfloat16)],
        in_specs=[pl.BlockSpec(memory_space=pl.ANY)] * 6,
        out_specs=[pl.BlockSpec(memory_space=pltpu.VMEM)] * 5,
        scratch_shapes=[
            pltpu.VMEM(tile, jnp.float32),
            pltpu.VMEM(tile, jnp.float32),
            pltpu.VMEM(tile, jnp.float32),
            pltpu.VMEM(tile, jnp.float32),
            pltpu.VMEM(tile, jnp.int32),
            pltpu.SMEM(tile, jnp.int32),
            pltpu.SMEM((512,), jnp.int32),
            pltpu.VMEM((2, 4, LANES), jnp.float32),
            pltpu.VMEM((2 * REACH, 4, LANES), jnp.float32),
            dma((7,)), dma((16,)), dma((16,)), dma((7,)), dma((7,)),
            dma((3,)), dma((3,)), dma((12,)), dma((12,)), dma((16,)), dma((16,)),
        ],
        compiler_params=pltpu.CompilerParams(collective_id=0, has_side_effects=True),
        name="lamb",
    )(
        master.reshape(tile), gradients.reshape(tile), first_moment.reshape(tile),
        second_moment.reshape(tile), segment_ids.reshape(tile), decay_mask,
    )
    new_master, new_first, new_second, scaled, weights = outs
    return (
        new_master.reshape(-1), new_first.reshape(-1), new_second.reshape(-1),
        scaled.reshape(-1), weights.reshape(-1),
    )


def solution(mesh):
    return jax.shard_map(
        shards,
        mesh=mesh,
        in_specs=(P("dp"), P("dp"), P("dp"), P("dp"), P("dp"), P()),
        out_specs=(P("dp"), P("dp"), P("dp"), P("dp"), P()),
        check_vma=False,
    )
```

time: 167 us -> 39.9 us (0.24)
  waiting for transfers between devices: 96.7 us -> 0 us
  blocking collectives: 44.9 us -> 0 us
  Pallas kernels: 0 us -> 33.1 us
  between operations: 16.1 us -> 0.65 us
  matrix products: 2.58 us -> 0 us
  other arithmetic: 1.93 us -> 0 us
    all_gather x1 -> x0, waiting for transfers between devices: 96.7 us -> none  [shards(): lax.all_gather(new_master.astype(jnp.bfloat16), DP, axis=0, tiled=True)]
    psum x4 -> x0, blocking collectives: 44.9 us -> none  [one_axis_at_a_time(): return functools.reduce(lax.psum, axes, value)]
    pallas_call x0 -> x1, Pallas kernels: none -> 33.1 us  [shards(): pl.pallas_call(kernel, out_shape=[f32, f32, f32, f32, jax.ShapeDtypeStruc...]
    unnamed x13, local copies, waits for them, and re-layouts: 2.96 us -> 5.65 us
    dot_general x6 -> x0, matrix products: 2.58 us -> none  [the longest x4 1.81 us: one_block(): jnp.dot(one_hot_block(block_ids, width), table, precision=lax.Precision.H...]
  transfers between devices with their start and end apart: 1 -> 0, of which waited for: 1 -> 0; matrix products, arithmetic and copies ran while one was open for 0% -> 0% of each run, Pallas kernels for 0% -> 0%
where the time goes in v1:
time: 39.9 us; the launch traced here: 39.5 us
  Pallas kernels  33.1 us (83%)
  local copies, waits for them, and re-layouts  5.65 us (14%)
  between operations  0.65 us (2%)
    pallas_call x1, Pallas kernels, shards(): pl.pallas_call(kernel, out_shape=[f32, f32, f32, f32, jax.ShapeDtypeStruc...  33.1 us
    unnamed x13, local copies, waits for them, and re-layouts  5.65 us

profile of v1, /device:TPU:1, one launch (start us, length us, event | category | flops | bytes accessed | tf_op | source)
XLA Modules:
  0.0 39.5 jit_solution(7845798705727661949)
XLA Ops:
  0.6 33.1 %lamb.1 = (f32[16,128]{1,0:T(8,128)}, f32[16,128]{1,0:T(8,128)}, f32[16,128]{1,0:T(8,128)}, f32[16,128]{1,0:T(8,128)}, bf16[4,8,4,2,16,128]{5,4,3,2,1,0:T(8,128)(2,1)}) custom-call(f32[16,128]{1,0:T(8,128)} %bitcast.15, f32[16,128]{1,0:T(8,128)} %bitcast.16, f32[16,128]{1,0:T(8,128)} %bitcast.17, f32[16,128]{1,0:T(8,128)} %bitcast.18, s32[16,128]{1,0:T(8,128)} %bitcast.19, ...), custom_call_target="tpu_custom_call" | custom-call | tf_op jit(solution)/shard_map/lamb/pallas_call | solution.py:256
  33.8 0.0 copy-start.3
  33.8 0.7 %copy-done.3 = f32[16,128]{1,0:T(8,128)S(1)} copy-done((f32[16,128]{1,0:T(8,128)S(1)}, f32[16,128]{1,0:T(8,128)}, u32[]{:S(2)}) %copy-start.3) | copy-done | bytes 8216
  34.5 0.0 copy-start.2
  34.5 0.6 %copy.16 = f32[2048]{0:T(1024)} copy(f32[2048]{0:T(1024)S(1)} %bitcast.14) | data formatting | bytes 16384
  35.1 0.1 copy-done.2
  35.2 0.0 copy-start.1
  35.2 0.6 %copy.17 = f32[2048]{0:T(1024)} copy(f32[2048]{0:T(1024)S(1)} %bitcast.13) | data formatting | bytes 16384
  35.8 0.1 copy-done.1
  35.9 0.0 copy-start
  35.9 0.6 %copy.18 = f32[2048]{0:T(1024)} copy(f32[2048]{0:T(1024)S(1)} %bitcast.12) | data formatting | bytes 16384
  36.5 0.1 copy-done
  36.6 0.6 %copy.19 = f32[2048]{0:T(1024)} copy(f32[2048]{0:T(1024)S(1)} %bitcast.11) | data formatting | bytes 16384
  37.2 2.3 %copy.20 = bf16[524288]{0:T(1024)(128)(2,1)} copy(bf16[524288]{0:T(1024)(128)(2,1)} %bitcast.10) | data formatting | bytes 2097152
Async XLA Ops:
  33.8 0.7 %copy-start.3 = (f32[16,128]{1,0:T(8,128)S(1)}, f32[16,128]{1,0:T(8,128)}, u32[]{:S(2)}) copy-start(f32[16,128]{1,0:T(8,128)} %get-tuple-element.10) | copy-start | bytes 24580
  34.5 0.7 %copy-start.2 = (f32[16,128]{1,0:T(8,128)S(1)}, f32[16,128]{1,0:T(8,128)}, u32[]{:S(2)}) copy-start(f32[16,128]{1,0:T(8,128)} %get-tuple-element.11) | copy-start | bytes 24580
  35.2 0.7 %copy-start.1 = (f32[16,128]{1,0:T(8,128)S(1)}, f32[16,128]{1,0:T(8,128)}, u32[]{:S(2)}) copy-start(f32[16,128]{1,0:T(8,128)} %get-tuple-element.12) | copy-start | bytes 24580
  35.9 0.7 %copy-start = (f32[16,128]{1,0:T(8,128)S(1)}, f32[16,128]{1,0:T(8,128)}, u32[]{:S(2)}) copy-start(f32[16,128]{1,0:T(8,128)} %get-tuple-element.13) | copy-start | bytes 24580
